TPU v7x, 32 devices: a whole 2x2x4 slice. The times are simulated.
32 devices in a mesh: lat: 16 (over z, x, core), tm: 2 (over y).
Axes of the slice: x: 2, y: 2, z: 4, core: 2. Of those that a mesh axis runs over, the one named last changes fastest.
Arguments:
- fields: bfloat16 [512, 64, 1024], P('lat', 'tm'), may hold values from -16 to 16
Outputs:
- covariance: float32 [64, 64], P('tm')
All inputs are finite; a program needn't handle non-finite values.
Results may differ from a plain program's by a relative error of at most 0.0003.
Values may be sent and summed in bfloat16 or wider, within the bound.
A program may use at most 64 MiB of HBM per device.

v0:
```python
import functools
import math

import jax
import jax.numpy as jnp
import numpy as np
from jax import lax
from jax.experimental import pallas as pl
from jax.experimental.pallas import tpu as pltpu
from jax.sharding import PartitionSpec as P

TRUNC = 341
LANES = 128
HALF = 64
PIECE = 8
PHASES = 3
MESH = pl.DeviceIdType.MESH


def phase_bounds(slots):
    length = -(-slots // PHASES)
    return [(low, min(low + length, slots)) for low in range(0, slots, length)]


def twiddle_table(device_total, slots, lon_count):
    longitude = np.arange(lon_count)
    parts = []
    for low, top in phase_bounds(slots):
        device = np.arange(device_total)[:, None]
        wave = (np.arange(low, top)[None, :] * device_total + device).reshape(-1, 1)
        phase = 2.0 * math.pi * ((wave * longitude) % lon_count) / lon_count
        active = (wave <= TRUNC) / math.sqrt(lon_count)
        parts += [np.cos(phase) * active, -np.sin(phase) * active]
    return np.concatenate(parts).astype(np.float32).astype(jnp.bfloat16)


def start_table(device_total, slots, slot_rows):
    table = np.zeros((device_total, slot_rows), np.float64)
    for device in range(device_total):
        for slot in range(slot_rows):
            order = min(slot, slots - 1) * device_total + device
            table[device, slot] = 0.5 * (
                math.log(0.5)
                + math.lgamma(order + 1.5)
                - math.lgamma(1.5)
                - math.lgamma(order + 1.0)
            )
    table = np.broadcast_to(table[:, :, None], (device_total, slot_rows, LANES))
    return table.astype(np.float32)


def needed_slots(lat_devices, device_total, slots, rows):
    counts = []
    order = np.arange(slots * device_total)
    rise = np.array(
        [math.lgamma(m + 1.5) - math.lgamma(1.5) - math.lgamma(m + 1.0) for m in order]
    )
    for device in range(lat_devices):
        lat = device * rows + np.arange(rows)
        sine = np.sin(math.pi * (lat + 0.5) / (lat_devices * rows))
        start = 0.5 * (math.log(0.5) + rise[:, None]) + order[:, None] * np.log(sine)[None, :]
        used = (start > -70.5) & (order <= TRUNC)[:, None]
        used = used.reshape(slots, -1).any(axis=1)
        counts.append(int(np.max(np.nonzero(used)[0])) + 1 if used.any() else 0)
    runs = []
    for device, count in enumerate(counts):
        if runs and runs[-1][2] == count:
            runs[-1][1] = device + 1
        else:
            runs.append([device, device + 1, count])
    return tuple(tuple(run) for run in runs)


def lat_table(lat_total, share):
    lat = np.arange(lat_total).reshape(lat_total // share, share).T.reshape(-1)
    theta = math.pi * (lat + 0.5) / lat_total
    table = np.stack([np.cos(theta), np.log(np.sin(theta)), math.pi * np.sin(theta) / lat_total])
    return table.reshape(3, lat_total // LANES, LANES).astype(np.float32)


def kernel(
    dims,
    runs,
    x_hbm,
    table_hbm,
    start_ref,
    lat_ref,
    out_ref,
    x_ref,
    table_ref,
    spread,
    outbox,
    inbox,
    legendre,
    gram_ref,
    local_gram,
    parts,
    own_sum,
    full,
    x_sem,
    table_sem,
    send_sem,
    recv_sem,
    part_send,
    part_recv,
    sum_send,
    sum_recv,
):
    lat_devices, tm_devices, rows, months, lon_count, slots, slot_rows, depth = dims
    device_total = lat_devices * tm_devices
    share = HALF // months
    high = rows // share
    lat_total = lat_devices * rows
    lat_groups = lat_total // LANES
    month_total = months * tm_devices
    pieces = month_total // PIECE
    stride = device_total // 2 // pieces
    first_owner = device_total // 4
    lat_me = lax.axis_index("lat")
    tm_me = lax.axis_index("tm")
    me = lat_me * tm_devices + tm_me

    phases = phase_bounds(slots)

    def each_peer(act):
        def row(lat):
            for tm in range(tm_devices):
                act(lat, tm)

        pl.loop(lat_me + 1, lat_devices)(row)
        pl.loop(0, lat_me)(row)
        for tm in range(tm_devices):

            @pl.when(tm_me != tm)
            def _():
                act(lat_me, tm)

    x_copy = pltpu.make_async_copy(x_hbm, x_ref, x_sem)
    x_copy.start()

    def table_copy(phase):
        low, top = phases[phase]
        span = pl.ds(2 * device_total * low, 2 * device_total * (top - low))
        return pltpu.make_async_copy(table_hbm.at[span], table_ref.at[span], table_sem.at[phase])

    for phase in range(len(phases)):
        table_copy(phase).start()

    barrier = pltpu.get_barrier_semaphore()
    each_peer(
        lambda lat, tm: pl.semaphore_signal(
            barrier, inc=1, device_id=(lat, tm), device_id_type=MESH
        )
    )

    for first, last, count in runs:
        if count < slots:

            @pl.loop(first * tm_devices, last * tm_devices)
            def _(source):
                inbox[source, count:] = jnp.zeros((slots - count, high, LANES), jnp.bfloat16)

    def transform(phase):
        low, top = phases[phase]
        group_rows = device_total * (top - low)
        lower = lax.broadcasted_iota(jnp.int32, (group_rows, LANES), 1) < HALF
        table_copy(phase).wait()
        values = lax.dot_general(
            table_ref[2 * device_total * low : 2 * device_total * top],
            x_ref[...],
            (((1,), (1,)), ((), ())),
            preferred_element_type=jnp.float32,
        )
        for block in range(rows * months // LANES):
            cosine = values[:group_rows, block * LANES : (block + 1) * LANES]
            sine = values[group_rows:, block * LANES : (block + 1) * LANES]
            even = jnp.where(lower, cosine, pltpu.roll(sine, HALF, 1))
            odd = jnp.where(lower, pltpu.roll(cosine, HALF, 1), sine)
            spread[pl.ds(2 * block, group_rows, stride=high), :] = even
            spread[pl.ds(2 * block + 1, group_rows, stride=high), :] = odd
        packed = spread[: group_rows * high].astype(jnp.bfloat16)
        outbox[:, low:top] = packed.reshape(device_total, top - low, high, LANES)

    def exchange(phase, count, lat, tm, source):
        low, top = phases[phase]
        span = pl.ds(low, min(count, top) - low)
        target = lat * tm_devices + tm
        return pltpu.make_async_remote_copy(
            src_ref=outbox.at[target, span],
            dst_ref=inbox.at[source, span],
            send_sem=send_sem.at[phase, target],
            recv_sem=recv_sem.at[phase, source],
            device_id=(lat, tm),
            device_id_type=MESH,
        )

    def each_send(phase, act):
        for first, last, count in runs:
            if count > phases[phase][0]:

                @pl.when((lat_me >= first) & (lat_me < last))
                def _():
                    each_peer(lambda lat, tm: act(exchange(phase, count, lat, tm, me)))

    x_copy.wait()
    for phase in range(len(phases)):
        transform(phase)
        if phase == 0:
            pl.semaphore_wait(barrier, device_total - 1)
        each_send(phase, lambda copy: copy.start())

    inbox[me] = outbox[me]

    halves = slot_rows // 8
    sub = lax.broadcasted_iota(jnp.int32, (8, LANES), 0)
    slot_of = [sub + 8 * half for half in range(halves)]
    order_int = [slot * device_total + me for slot in slot_of]
    order = [value.astype(jnp.float32) for value in order_int]
    cosine_lat = [jnp.broadcast_to(lat_ref[0, pl.ds(g, 1), :], (8, LANES)) for g in range(lat_groups)]
    current = []
    scale = []
    for half in range(halves):
        factor = jnp.where(order_int[half] > 0, math.sqrt(2.0), 1.0)
        for g in range(lat_groups):
            log_start = (
                start_ref[me, pl.ds(8 * half, 8), :]
                + order[half] * jnp.broadcast_to(lat_ref[1, pl.ds(g, 1), :], (8, LANES))
            )
            taper = jnp.clip((log_start + 70.0) / 10.0, 0.0, 1.0)
            current.append(jnp.exp(jnp.maximum(log_start, -80.0)) * taper)
            scale.append(factor * jnp.broadcast_to(lat_ref[2, pl.ds(g, 1), :], (8, LANES)))

    def store(offset, values):
        for half in range(halves):
            keep = (order_int[half] + offset <= TRUNC) & (slot_of[half] < slots)
            for g in range(lat_groups):
                index = half * lat_groups + g
                value = jnp.where(keep, values[index] * scale[index], 0.0)
                legendre[g, pl.ds(8 * half * depth + offset, 8, stride=depth), :] = value

    store(0, current)

    def advance(offset, carry):
        now, before, backs = carry
        real = lax.convert_element_type(offset, jnp.float32)
        following = []
        next_backs = []
        for half in range(halves):
            degree = order[half] + real
            ratio = (4.0 * degree * degree - 1.0) / (real * (order[half] + degree))
            top = jnp.sqrt(ratio)
            next_backs.append(1.0 / top)
            for g in range(lat_groups):
                index = half * lat_groups + g
                following.append(
                    top * (cosine_lat[g] * now[index] - backs[half] * before[index])
                )
        store(offset, following)
        return following, now, next_backs

    zero = jnp.zeros((8, LANES), jnp.float32)
    lax.fori_loop(
        1,
        depth,
        advance,
        (current, [zero] * len(current), [zero] * halves),
        unroll=7,
    )

    per_share = lat_groups // share
    width = tm_devices * LANES
    share_of = lax.broadcasted_iota(jnp.int32, (depth, width), 1) % HALF // months
    gram_ref[...] = jnp.zeros_like(gram_ref)

    def add_slot(slot):
        received = jnp.concatenate(
            [
                jnp.concatenate(
                    [
                        inbox[lat_device * tm_devices + tm, slot]
                        for lat_device in range(lat_devices)
                    ],
                    axis=0,
                )
                for tm in range(tm_devices)
            ],
            axis=1,
        )
        first = pl.multiple_of(slot * depth, 8)
        merged = None
        for part in range(share):
            basis = jnp.concatenate(
                [
                    legendre[part * per_share + g, pl.ds(first, depth), :].astype(jnp.bfloat16)
                    for g in range(per_share)
                ],
                axis=1,
            )
            product = jnp.dot(basis, received, preferred_element_type=jnp.float32)
            merged = product if part == 0 else jnp.where(share_of == part, product, merged)
        total = merged
        for part in range(1, share):
            total = total + pltpu.roll(merged, width - part * months, 1)
        coefficients = jnp.where(share_of == 0, total, 0.0).astype(jnp.bfloat16)
        gram_ref[...] += lax.dot_general(
            coefficients,
            coefficients,
            (((0,), (0,)), ((), ())),
            preferred_element_type=jnp.float32,
        )

    for phase, (low, top) in enumerate(phases):
        for first, last, count in runs:
            if count > low:

                @pl.loop(first, last)
                def _(lat):
                    for tm in range(tm_devices):
                        source = lat * tm_devices + tm

                        @pl.when(source != me)
                        def _():
                            exchange(phase, count, lat, tm, source).wait_recv()

        pl.loop(low, top)(add_slot)

    gram = None
    for part in range(2):
        across = jnp.concatenate(
            [
                gram_ref[pl.ds(tm * LANES + part * HALF, months), :]
                for tm in range(tm_devices)
            ],
            axis=0,
        )
        block = jnp.concatenate(
            [
                across[:, tm * LANES + part * HALF : tm * LANES + part * HALF + months]
                for tm in range(tm_devices)
            ],
            axis=1,
        )
        gram = block if gram is None else gram + block
    local_gram[...] = gram.reshape(pieces, PIECE, month_total)

    lat_step = stride // tm_devices
    first_lat = first_owner // tm_devices

    def owner(piece):
        return first_lat + piece * lat_step

    def send_part(piece, source):
        return pltpu.make_async_remote_copy(
            src_ref=local_gram.at[piece],
            dst_ref=parts.at[source],
            send_sem=part_send.at[piece],
            recv_sem=part_recv.at[source],
            device_id=(owner(piece), 0),
            device_id_type=MESH,
        )

    def send_sum(piece, lat, tm):
        return pltpu.make_async_remote_copy(
            src_ref=own_sum,
            dst_ref=full.at[piece],
            send_sem=sum_send.at[lat * tm_devices + tm],
            recv_sem=sum_recv.at[piece],
            device_id=(lat, tm),
            device_id_type=MESH,
        )

    def not_mine(piece):
        return (owner(piece) != lat_me) | (tm_me != 0)

    @pl.loop(0, pieces)
    def _(piece):
        @pl.when(not_mine(piece))
        def _():
            send_part(piece, me).start()

    for phase in range(len(phases)):
        each_send(phase, lambda copy: copy.wait_send())

    @pl.loop(0, pieces)
    def _(piece):
        @pl.when((owner(piece) == lat_me) & (tm_me == 0))
        def _():
            parts[me] = local_gram[piece]
            each_peer(lambda lat, tm: send_part(piece, lat * tm_devices + tm).wait_recv())
            total = jnp.sum(parts[...], axis=0)
            own_sum[...] = total
            full[piece] = total
            each_peer(lambda lat, tm: send_sum(piece, lat, tm).start())

    @pl.loop(0, pieces)
    def _(piece):
        @pl.when(not_mine(piece))
        def _():
            send_sum(piece, lat_me, tm_me).wait_recv()

    gram = full[...].reshape(month_total, month_total)
    on_diagonal = lax.broadcasted_iota(jnp.int32, gram.shape, 0) == lax.broadcasted_iota(
        jnp.int32, gram.shape, 1
    )
    trace = jnp.sum(jnp.where(on_diagonal, gram, 0.0))
    mine = full[pl.ds(tm_me * (months // PIECE), months // PIECE)].reshape(months, month_total)
    out_ref[...] = month_total * mine / (trace + 1e-06)

    @pl.loop(0, pieces)
    def _(piece):
        @pl.when(not_mine(piece))
        def _():
            send_part(piece, me).wait_send()

        @pl.when((owner(piece) == lat_me) & (tm_me == 0))
        def _():
            each_peer(lambda lat, tm: send_sum(piece, lat, tm).wait_send())


def solution(mesh):
    lat_devices = mesh.shape["lat"]
    tm_devices = mesh.shape["tm"]
    device_total = lat_devices * tm_devices
    slots = -(-(TRUNC + 1) // device_total)
    slot_rows = -(-slots // 8) * 8
    depth = -(-(TRUNC + 1) // 8) * 8

    def local(fields):
        rows, months, lon_count = fields.shape
        month_total = months * tm_devices
        lat_total = rows * lat_devices
        share = HALF // months
        high = rows // share
        pieces = month_total // PIECE
        width = tm_devices * LANES
        dims = (lat_devices, tm_devices, rows, months, lon_count, slots, slot_rows, depth)
        table = jnp.asarray(twiddle_table(device_total, slots, lon_count))
        starts = jnp.asarray(start_table(device_total, slots, slot_rows))
        lats = jnp.asarray(lat_table(lat_total, share))
        runs = needed_slots(lat_devices, device_total, slots, rows)
        phases = phase_bounds(slots)
        longest = max(top - low for low, top in phases)
        hbm = pl.BlockSpec(memory_space=pl.ANY)
        vmem = pl.BlockSpec(memory_space=pltpu.VMEM)
        dma = pltpu.SemaphoreType.DMA
        return pl.pallas_call(
            functools.partial(kernel, dims, runs),
            out_shape=jax.ShapeDtypeStruct((months, month_total), jnp.float32),
            in_specs=[hbm, hbm, vmem, vmem],
            out_specs=vmem,
            scratch_shapes=[
                pltpu.VMEM((rows * months, lon_count), jnp.bfloat16),
                pltpu.VMEM(table.shape, jnp.bfloat16),
                pltpu.VMEM((device_total * longest * high, LANES), jnp.float32),
                pltpu.VMEM((device_total, slots, high, LANES), jnp.bfloat16),
                pltpu.VMEM((device_total, slots, high, LANES), jnp.bfloat16),
                pltpu.VMEM((lat_total // LANES, slot_rows * depth, LANES), jnp.float32),
                pltpu.VMEM((width, width), jnp.float32),
                pltpu.VMEM((pieces, PIECE, month_total), jnp.float32),
                pltpu.VMEM((device_total, PIECE, month_total), jnp.float32),
                pltpu.VMEM((PIECE, month_total), jnp.float32),
                pltpu.VMEM((pieces, PIECE, month_total), jnp.float32),
                dma,
                dma((len(phases),)),
                dma((len(phases), device_total)),
                dma((len(phases), device_total)),
                dma((pieces,)),
                dma((device_total,)),
                dma((device_total,)),
                dma((pieces,)),
            ],
            compiler_params=pltpu.CompilerParams(
                collective_id=0, has_side_effects=True, vmem_limit_bytes=60 * 1024 * 1024
            ),
        )(fields.reshape(rows * months, lon_count), table, starts, lats)

    return jax.shard_map(
        local, mesh=mesh, in_specs=(P("lat", "tm", None),), out_specs=P("tm", None), check_vma=False
    )
```

profile of v0, /device:TPU:0, one launch (start us, length us, event | category | flops | bytes accessed | tf_op | source)
XLA Modules:
  0.0 46.6 jit_solution(2618711879356109698)
XLA Ops:
  0.0 45.2 %shard_map.46 = f32[32,64]{1,0:T(8,128)} custom-call(bf16[1024,1024]{1,0:T(8,128)(2,1)} %bitcast.1, bf16[704,1024]{1,0:T(8,128)(2,1)} %constant.6.clone.table_hbm, f32[32,16,128]{2,1,0:T(8,128)} %constant.7.clone.start_ref, f32[3,4,128]{2,1,0:T(4,128)} %constant.8.clone.lat_ref), custom_call_target="tpu_custom_call" | custom-call | tf_op jit(solution)/shard_map/pallas_call | solution.py:446
  45.3 1.3 %copy.6 = f32[32,64]{1,0:T(8,128)} copy(f32[32,64]{1,0:T(8,128)} %shard_map.46) | data formatting | bytes 16384
where the time goes:
time: 46.8 us; the launch traced here: 46.6 us
  Pallas kernels  45.2 us (97%)
  local copies, waits for them, and re-layouts  1.32 us (3%)
    pallas_call x1, Pallas kernels, local(): pl.pallas_call(functools.partial(kernel, dims, runs), out_shape=jax.Shape...  45.2 us
    unnamed x1, local copies, waits for them, and re-layouts  1.32 us

commit v1 on v0

--- a/solution.py
+++ b/solution.py
@@ -19,26 +19,41 @@
 
 def phase_bounds(slots):
     length = -(-slots // PHASES)
-    return [(low, min(low + length, slots)) for low in range(0, slots, length)]
-
-
-def twiddle_table(device_total, slots, lon_count):
+    bounds = [(low, min(low + length, slots)) for low in range(0, slots, length)]
+    low, top = bounds.pop()
+    if top - low > 1:
+        bounds.append((low, top - 1))
+    return bounds + [(top - 1, top)]
+
+
+def rank_of(lat, tm, lat_devices, tm_devices):
+    hemisphere = lat_devices // 2
+    return ((lat % hemisphere) * tm_devices + tm) * 2 + lat // hemisphere
+
+
+def ranks(lat_devices, tm_devices):
+    device = np.arange(lat_devices * tm_devices)
+    return rank_of(device // tm_devices, device % tm_devices, lat_devices, tm_devices)
+
+
+def twiddle_table(rank, slots, lon_count):
+    device_total = len(rank)
     longitude = np.arange(lon_count)
     parts = []
     for low, top in phase_bounds(slots):
-        device = np.arange(device_total)[:, None]
-        wave = (np.arange(low, top)[None, :] * device_total + device).reshape(-1, 1)
+        wave = (np.arange(low, top)[None, :] * device_total + rank[:, None]).reshape(-1, 1)
         phase = 2.0 * math.pi * ((wave * longitude) % lon_count) / lon_count
         active = (wave <= TRUNC) / math.sqrt(lon_count)
         parts += [np.cos(phase) * active, -np.sin(phase) * active]
     return np.concatenate(parts).astype(np.float32).astype(jnp.bfloat16)
 
 
-def start_table(device_total, slots, slot_rows):
+def start_table(rank, slots, slot_rows):
+    device_total = len(rank)
     table = np.zeros((device_total, slot_rows), np.float64)
     for device in range(device_total):
         for slot in range(slot_rows):
-            order = min(slot, slots - 1) * device_total + device
+            order = min(slot, slots - 1) * device_total + int(rank[device])
             table[device, slot] = 0.5 * (
                 math.log(0.5)
                 + math.lgamma(order + 1.5)
@@ -49,7 +64,7 @@
     return table.astype(np.float32)
 
 
-def needed_slots(lat_devices, device_total, slots, rows):
+def needed_slots(lat_devices, device_total, slots, rows, bands):
     counts = []
     order = np.arange(slots * device_total)
     rise = np.array(
@@ -60,8 +75,13 @@
         sine = np.sin(math.pi * (lat + 0.5) / (lat_devices * rows))
         start = 0.5 * (math.log(0.5) + rise[:, None]) + order[:, None] * np.log(sine)[None, :]
         used = (start > -70.5) & (order <= TRUNC)[:, None]
-        used = used.reshape(slots, -1).any(axis=1)
-        counts.append(int(np.max(np.nonzero(used)[0])) + 1 if used.any() else 0)
+        used = used.reshape(slots, device_total, bands, -1).any(axis=(1, 3))
+        counts.append(
+            tuple(
+                int(np.max(np.nonzero(used[:, band])[0])) + 1 if used[:, band].any() else 0
+                for band in range(bands)
+            )
+        )
     runs = []
     for device, count in enumerate(counts):
         if runs and runs[-1][2] == count:
@@ -83,11 +103,13 @@
     runs,
     x_hbm,
     table_hbm,
-    start_ref,
-    lat_ref,
+    start_hbm,
+    lat_hbm,
     out_ref,
     x_ref,
     table_ref,
+    start_ref,
+    lat_ref,
     spread,
     outbox,
     inbox,
@@ -99,12 +121,10 @@
     full,
     x_sem,
     table_sem,
+    small_sem,
     send_sem,
     recv_sem,
-    part_send,
-    part_recv,
-    sum_send,
-    sum_recv,
+    tail_sem,
 ):
     lat_devices, tm_devices, rows, months, lon_count, slots, slot_rows, depth = dims
     device_total = lat_devices * tm_devices
@@ -114,11 +134,10 @@
     lat_groups = lat_total // LANES
     month_total = months * tm_devices
     pieces = month_total // PIECE
-    stride = device_total // 2 // pieces
-    first_owner = device_total // 4
     lat_me = lax.axis_index("lat")
     tm_me = lax.axis_index("tm")
     me = lat_me * tm_devices + tm_me
+    rank_me = rank_of(lat_me, tm_me, lat_devices, tm_devices)
 
     phases = phase_bounds(slots)
 
@@ -135,6 +154,13 @@
             def _():
                 act(lat_me, tm)
 
+    barrier = pltpu.get_barrier_semaphore()
+    each_peer(
+        lambda lat, tm: pl.semaphore_signal(
+            barrier, inc=1, device_id=(lat, tm), device_id_type=MESH
+        )
+    )
+
     x_copy = pltpu.make_async_copy(x_hbm, x_ref, x_sem)
     x_copy.start()
 
@@ -146,19 +172,62 @@
     for phase in range(len(phases)):
         table_copy(phase).start()
 
-    barrier = pltpu.get_barrier_semaphore()
-    each_peer(
-        lambda lat, tm: pl.semaphore_signal(
-            barrier, inc=1, device_id=(lat, tm), device_id_type=MESH
-        )
-    )
-
-    for first, last, count in runs:
-        if count < slots:
-
-            @pl.loop(first * tm_devices, last * tm_devices)
-            def _(source):
-                inbox[source, count:] = jnp.zeros((slots - count, high, LANES), jnp.bfloat16)
+    start_copy = pltpu.make_async_copy(start_hbm.at[me], start_ref, small_sem.at[0])
+    start_copy.start()
+    lat_copy = pltpu.make_async_copy(lat_hbm, lat_ref, small_sem.at[1])
+    lat_copy.start()
+
+    bands = len(runs[0][2])
+    band_rows = high // bands
+    for first, last, counts in runs:
+        for band, count in enumerate(counts):
+            if count < slots:
+
+                @pl.loop(first * tm_devices, last * tm_devices)
+                def _(source):
+                    for slot in range(count, slots):
+                        inbox[source, slot * bands + band] = jnp.zeros(
+                            (band_rows, LANES), jnp.bfloat16
+                        )
+
+    def pieces_of(phase, counts):
+        low, top = phases[phase]
+        found = []
+        shared = min(min(counts), top)
+        if shared > low:
+            found.append((low * bands, (shared - low) * bands))
+        for band, count in enumerate(counts):
+            for slot in range(max(low, min(counts)), min(count, top)):
+                found.append((slot * bands + band, 1))
+        return found
+
+    def blocks_of(phase, counts):
+        return sum(length for first, length in pieces_of(phase, counts))
+
+    def arriving(phase):
+        return sum(
+            (last - first) * tm_devices * blocks_of(phase, counts) for first, last, counts in runs
+        )
+
+    def holds(phase, lat, tm):
+        low, top = phases[phase]
+        rank = rank_of(lat, tm, lat_devices, tm_devices)
+        return low * device_total + rank <= TRUNC
+
+    def holders(phase):
+        return min(TRUNC + 1 - phases[phase][0] * device_total, device_total)
+
+    def wait_blocks(semaphore, count):
+        if count:
+            span = spread.at[pl.ds(0, count * band_rows // 2)]
+            pltpu.make_async_copy(span, span, semaphore).wait()
+
+    def each_class(act):
+        for first, last, counts in runs:
+
+            @pl.when((lat_me >= first) & (lat_me < last))
+            def _():
+                act(counts)
 
     def transform(phase):
         low, top = phases[phase]
@@ -179,42 +248,83 @@
             spread[pl.ds(2 * block, group_rows, stride=high), :] = even
             spread[pl.ds(2 * block + 1, group_rows, stride=high), :] = odd
         packed = spread[: group_rows * high].astype(jnp.bfloat16)
-        outbox[:, low:top] = packed.reshape(device_total, top - low, high, LANES)
-
-    def exchange(phase, count, lat, tm, source):
-        low, top = phases[phase]
-        span = pl.ds(low, min(count, top) - low)
-        target = lat * tm_devices + tm
+        outbox[:, low * bands : top * bands] = packed.reshape(
+            device_total, (top - low) * bands, band_rows, LANES
+        )
+
+    def exchange(phase, piece, lat, tm):
+        span = pl.ds(*piece)
         return pltpu.make_async_remote_copy(
-            src_ref=outbox.at[target, span],
-            dst_ref=inbox.at[source, span],
-            send_sem=send_sem.at[phase, target],
-            recv_sem=recv_sem.at[phase, source],
+            src_ref=outbox.at[lat * tm_devices + tm, span],
+            dst_ref=inbox.at[me, span],
+            send_sem=send_sem.at[phase],
+            recv_sem=recv_sem.at[phase],
             device_id=(lat, tm),
             device_id_type=MESH,
         )
 
-    def each_send(phase, act):
-        for first, last, count in runs:
-            if count > phases[phase][0]:
-
-                @pl.when((lat_me >= first) & (lat_me < last))
-                def _():
-                    each_peer(lambda lat, tm: act(exchange(phase, count, lat, tm, me)))
-
-    x_copy.wait()
+    all_hold = [holders(phase) == device_total for phase in range(len(phases))]
+
+    def send(phase):
+        def send_class(counts):
+            def send_to(lat, tm):
+                def go():
+                    for piece in pieces_of(phase, counts):
+                        exchange(phase, piece, lat, tm).start()
+
+                if all_hold[phase]:
+                    go()
+                else:
+                    pl.when(holds(phase, lat, tm))(go)
+
+            if blocks_of(phase, counts):
+                each_peer(send_to)
+
+        each_class(send_class)
+
+    def wait_sent(phase):
+        def wait_class(counts):
+            length = blocks_of(phase, counts)
+            if all_hold[phase]:
+                wait_blocks(send_sem.at[phase], (device_total - 1) * length)
+            elif length:
+                held = holds(phase, lat_me, tm_me)
+                pl.when(held)(
+                    lambda: wait_blocks(send_sem.at[phase], (holders(phase) - 1) * length)
+                )
+                pl.when(jnp.logical_not(held))(
+                    lambda: wait_blocks(send_sem.at[phase], holders(phase) * length)
+                )
+
+        each_class(wait_class)
+
+    def wait_arrived(phase):
+        each_class(
+            lambda counts: wait_blocks(
+                recv_sem.at[phase], arriving(phase) - blocks_of(phase, counts)
+            )
+        )
+
+    with jax.named_scope("xwait"):
+        x_copy.wait()
     for phase in range(len(phases)):
-        transform(phase)
+        with jax.named_scope(f"transform{phase}"):
+            transform(phase)
         if phase == 0:
-            pl.semaphore_wait(barrier, device_total - 1)
-        each_send(phase, lambda copy: copy.start())
+            with jax.named_scope("barrier"):
+                pl.semaphore_wait(barrier, device_total - 1)
+        with jax.named_scope(f"send{phase}"):
+            send(phase)
 
     inbox[me] = outbox[me]
+
+    start_copy.wait()
+    lat_copy.wait()
 
     halves = slot_rows // 8
     sub = lax.broadcasted_iota(jnp.int32, (8, LANES), 0)
     slot_of = [sub + 8 * half for half in range(halves)]
-    order_int = [slot * device_total + me for slot in slot_of]
+    order_int = [slot * device_total + rank_me for slot in slot_of]
     order = [value.astype(jnp.float32) for value in order_int]
     cosine_lat = [jnp.broadcast_to(lat_ref[0, pl.ds(g, 1), :], (8, LANES)) for g in range(lat_groups)]
     current = []
@@ -223,7 +333,7 @@
         factor = jnp.where(order_int[half] > 0, math.sqrt(2.0), 1.0)
         for g in range(lat_groups):
             log_start = (
-                start_ref[me, pl.ds(8 * half, 8), :]
+                start_ref[pl.ds(8 * half, 8), :]
                 + order[half] * jnp.broadcast_to(lat_ref[1, pl.ds(g, 1), :], (8, LANES))
             )
             taper = jnp.clip((log_start + 70.0) / 10.0, 0.0, 1.0)
@@ -259,13 +369,14 @@
         return following, now, next_backs
 
     zero = jnp.zeros((8, LANES), jnp.float32)
-    lax.fori_loop(
-        1,
-        depth,
-        advance,
-        (current, [zero] * len(current), [zero] * halves),
-        unroll=7,
-    )
+    with jax.named_scope("legendre"):
+        lax.fori_loop(
+            1,
+            depth,
+            advance,
+            (current, [zero] * len(current), [zero] * halves),
+            unroll=7,
+        )
 
     per_share = lat_groups // share
     width = tm_devices * LANES
@@ -277,7 +388,9 @@
             [
                 jnp.concatenate(
                     [
-                        inbox[lat_device * tm_devices + tm, slot]
+                        inbox[lat_device * tm_devices + tm, pl.ds(slot * bands, bands)].reshape(
+                            high, LANES
+                        )
                         for lat_device in range(lat_devices)
                     ],
                     axis=0,
@@ -309,20 +422,18 @@
             preferred_element_type=jnp.float32,
         )
 
-    for phase, (low, top) in enumerate(phases):
-        for first, last, count in runs:
-            if count > low:
-
-                @pl.loop(first, last)
-                def _(lat):
-                    for tm in range(tm_devices):
-                        source = lat * tm_devices + tm
-
-                        @pl.when(source != me)
-                        def _():
-                            exchange(phase, count, lat, tm, source).wait_recv()
-
-        pl.loop(low, top)(add_slot)
+    def finish(phase):
+        low, top = phases[phase]
+        with jax.named_scope(f"recv{phase}"):
+            wait_arrived(phase)
+        with jax.named_scope(f"slots{phase}"):
+            pl.loop(low, top)(add_slot)
+
+    for phase in range(len(phases)):
+        if all_hold[phase]:
+            finish(phase)
+        else:
+            pl.when(holds(phase, lat_me, tm_me))(functools.partial(finish, phase))
 
     gram = None
     for part in range(2):
@@ -343,19 +454,24 @@
         gram = block if gram is None else gram + block
     local_gram[...] = gram.reshape(pieces, PIECE, month_total)
 
-    lat_step = stride // tm_devices
-    first_lat = first_owner // tm_devices
+    owner_lats = -(-pieces // tm_devices)
+    lat_step = max(lat_devices // 2 // owner_lats, 1)
+    first_lat = lat_devices // 4 + lat_step - 1
 
     def owner(piece):
-        return first_lat + piece * lat_step
+        return (first_lat + (piece // tm_devices) * lat_step, piece % tm_devices)
+
+    def mine(piece):
+        lat, tm = owner(piece)
+        return (lat == lat_me) & (tm == tm_me)
 
     def send_part(piece, source):
         return pltpu.make_async_remote_copy(
             src_ref=local_gram.at[piece],
             dst_ref=parts.at[source],
-            send_sem=part_send.at[piece],
-            recv_sem=part_recv.at[source],
-            device_id=(owner(piece), 0),
+            send_sem=tail_sem.at[0],
+            recv_sem=tail_sem.at[1],
+            device_id=owner(piece),
             device_id_type=MESH,
         )
 
@@ -363,14 +479,27 @@
         return pltpu.make_async_remote_copy(
             src_ref=own_sum,
             dst_ref=full.at[piece],
-            send_sem=sum_send.at[lat * tm_devices + tm],
-            recv_sem=sum_recv.at[piece],
+            send_sem=tail_sem.at[2],
+            recv_sem=tail_sem.at[3],
             device_id=(lat, tm),
             device_id_type=MESH,
         )
 
     def not_mine(piece):
-        return (owner(piece) != lat_me) | (tm_me != 0)
+        return jnp.logical_not(mine(piece))
+
+    owns_any = (
+        (lat_me >= first_lat)
+        & ((lat_me - first_lat) % lat_step == 0)
+        & ((lat_me - first_lat) // lat_step * tm_devices + tm_me < pieces)
+    )
+
+    def wait_refs(index, ref):
+        pltpu.make_async_copy(ref, ref, tail_sem.at[index]).wait()
+
+    def wait_pieces(index, ref):
+        pl.when(owns_any)(lambda: wait_refs(index, ref.at[pl.ds(0, pieces - 1)]))
+        pl.when(jnp.logical_not(owns_any))(lambda: wait_refs(index, ref))
 
     @pl.loop(0, pieces)
     def _(piece):
@@ -378,43 +507,42 @@
         def _():
             send_part(piece, me).start()
 
-    for phase in range(len(phases)):
-        each_send(phase, lambda copy: copy.wait_send())
-
-    @pl.loop(0, pieces)
-    def _(piece):
-        @pl.when((owner(piece) == lat_me) & (tm_me == 0))
+    with jax.named_scope("waitsend"):
+        for phase in range(len(phases)):
+            wait_sent(phase)
+
+    with jax.named_scope("owner"):
+
+        @pl.loop(0, pieces)
+        def _(piece):
+            @pl.when(mine(piece))
+            def _():
+                parts[me] = local_gram[piece]
+                wait_refs(1, parts.at[pl.ds(0, device_total - 1)])
+                total = jnp.sum(parts[...], axis=0)
+                own_sum[...] = total
+                full[piece] = total
+                each_peer(lambda lat, tm: send_sum(piece, lat, tm).start())
+
+    with jax.named_scope("waitsum"):
+
+        wait_pieces(3, full)
+
+    with jax.named_scope("norm"):
+        gram = full[...].reshape(month_total, month_total)
+        on_diagonal = lax.broadcasted_iota(jnp.int32, gram.shape, 0) == lax.broadcasted_iota(
+            jnp.int32, gram.shape, 1
+        )
+        trace = jnp.sum(jnp.where(on_diagonal, gram, 0.0))
+        here = full[pl.ds(tm_me * (months // PIECE), months // PIECE)].reshape(months, month_total)
+        out_ref[...] = month_total * here / (trace + 1e-06)
+
+    with jax.named_scope("drain"):
+        wait_pieces(0, local_gram)
+
+        @pl.when(owns_any)
         def _():
-            parts[me] = local_gram[piece]
-            each_peer(lambda lat, tm: send_part(piece, lat * tm_devices + tm).wait_recv())
-            total = jnp.sum(parts[...], axis=0)
-            own_sum[...] = total
-            full[piece] = total
-            each_peer(lambda lat, tm: send_sum(piece, lat, tm).start())
-
-    @pl.loop(0, pieces)
-    def _(piece):
-        @pl.when(not_mine(piece))
-        def _():
-            send_sum(piece, lat_me, tm_me).wait_recv()
-
-    gram = full[...].reshape(month_total, month_total)
-    on_diagonal = lax.broadcasted_iota(jnp.int32, gram.shape, 0) == lax.broadcasted_iota(
-        jnp.int32, gram.shape, 1
-    )
-    trace = jnp.sum(jnp.where(on_diagonal, gram, 0.0))
-    mine = full[pl.ds(tm_me * (months // PIECE), months // PIECE)].reshape(months, month_total)
-    out_ref[...] = month_total * mine / (trace + 1e-06)
-
-    @pl.loop(0, pieces)
-    def _(piece):
-        @pl.when(not_mine(piece))
-        def _():
-            send_part(piece, me).wait_send()
-
-        @pl.when((owner(piece) == lat_me) & (tm_me == 0))
-        def _():
-            each_peer(lambda lat, tm: send_sum(piece, lat, tm).wait_send())
+            wait_refs(2, parts.at[pl.ds(0, device_total - 1)])
 
 
 def solution(mesh):
@@ -434,10 +562,12 @@
         pieces = month_total // PIECE
         width = tm_devices * LANES
         dims = (lat_devices, tm_devices, rows, months, lon_count, slots, slot_rows, depth)
-        table = jnp.asarray(twiddle_table(device_total, slots, lon_count))
-        starts = jnp.asarray(start_table(device_total, slots, slot_rows))
+        rank = ranks(lat_devices, tm_devices)
+        table = jnp.asarray(twiddle_table(rank, slots, lon_count))
+        starts = jnp.asarray(start_table(rank, slots, slot_rows))
         lats = jnp.asarray(lat_table(lat_total, share))
-        runs = needed_slots(lat_devices, device_total, slots, rows)
+        bands = 2 if high % 16 == 0 else 1
+        runs = needed_slots(lat_devices, device_total, slots, rows, bands)
         phases = phase_bounds(slots)
         longest = max(top - low for low, top in phases)
         hbm = pl.BlockSpec(memory_space=pl.ANY)
@@ -446,14 +576,16 @@
         return pl.pallas_call(
             functools.partial(kernel, dims, runs),
             out_shape=jax.ShapeDtypeStruct((months, month_total), jnp.float32),
-            in_specs=[hbm, hbm, vmem, vmem],
+            in_specs=[hbm, hbm, hbm, hbm],
             out_specs=vmem,
             scratch_shapes=[
                 pltpu.VMEM((rows * months, lon_count), jnp.bfloat16),
                 pltpu.VMEM(table.shape, jnp.bfloat16),
+                pltpu.VMEM(starts.shape[1:], jnp.float32),
+                pltpu.VMEM(lats.shape, jnp.float32),
                 pltpu.VMEM((device_total * longest * high, LANES), jnp.float32),
-                pltpu.VMEM((device_total, slots, high, LANES), jnp.bfloat16),
-                pltpu.VMEM((device_total, slots, high, LANES), jnp.bfloat16),
+                pltpu.VMEM((device_total, slots * bands, high // bands, LANES), jnp.bfloat16),
+                pltpu.VMEM((device_total, slots * bands, high // bands, LANES), jnp.bfloat16),
                 pltpu.VMEM((lat_total // LANES, slot_rows * depth, LANES), jnp.float32),
                 pltpu.VMEM((width, width), jnp.float32),
                 pltpu.VMEM((pieces, PIECE, month_total), jnp.float32),
@@ -462,12 +594,10 @@
                 pltpu.VMEM((pieces, PIECE, month_total), jnp.float32),
                 dma,
                 dma((len(phases),)),
-                dma((len(phases), device_total)),
-                dma((len(phases), device_total)),
-                dma((pieces,)),
-                dma((device_total,)),
-                dma((device_total,)),
-                dma((pieces,)),
+                dma((2,)),
+                dma((len(phases),)),
+                dma((len(phases),)),
+                dma((4,)),
             ],
             compiler_params=pltpu.CompilerParams(
                 collective_id=0, has_side_effects=True, vmem_limit_bytes=60 * 1024 * 1024

time: 46.8 us -> 41.3 us (0.88)
  Pallas kernels: 45.2 us -> 39.7 us
    pallas_call x1, Pallas kernels: 45.2 us -> 39.7 us  [local(): pl.pallas_call(functools.partial(kernel, dims, runs), out_shape=jax.Shape...]
where the time goes in v1:
time: 41.3 us; the launch traced here: 41.1 us
  Pallas kernels  39.7 us (96%)
  local copies, waits for them, and re-layouts  1.32 us (3%)
    pallas_call x1, Pallas kernels, local(): pl.pallas_call(functools.partial(kernel, dims, runs), out_shape=jax.Shape...  39.7 us
    unnamed x1, local copies, waits for them, and re-layouts  1.32 us

profile of v1, /device:TPU:0, one launch (start us, length us, event | category | flops | bytes accessed | tf_op | source)
XLA Modules:
  0.0 41.1 jit_solution(1540731792148448455)
XLA Ops:
  0.0 39.7 %shard_map.46 = f32[32,64]{1,0:T(8,128)} custom-call(bf16[1024,1024]{1,0:T(8,128)(2,1)} %bitcast.1, bf16[704,1024]{1,0:T(8,128)(2,1)} %constant.6.clone.table_hbm, f32[32,16,128]{2,1,0:T(8,128)} %constant.7.clone.start_hbm, f32[3,4,128]{2,1,0:T(4,128)} %constant.8.clone.lat_hbm), custom_call_target="tpu_custom_call" | custom-call | tf_op jit(solution)/shard_map/pallas_call | solution.py:576
  39.7 1.3 %copy.6 = f32[32,64]{1,0:T(8,128)} copy(f32[32,64]{1,0:T(8,128)} %shard_map.46) | data formatting | bytes 16384

commit v2 on v1

--- a/solution.py
+++ b/solution.py
@@ -19,11 +19,7 @@
 
 def phase_bounds(slots):
     length = -(-slots // PHASES)
-    bounds = [(low, min(low + length, slots)) for low in range(0, slots, length)]
-    low, top = bounds.pop()
-    if top - low > 1:
-        bounds.append((low, top - 1))
-    return bounds + [(top - 1, top)]
+    return [(low, min(low + length, slots)) for low in range(0, slots, length)]
 
 
 def rank_of(lat, tm, lat_devices, tm_devices):
@@ -190,8 +186,27 @@
                             (band_rows, LANES), jnp.bfloat16
                         )
 
-    def pieces_of(phase, counts):
+    last_order = (slots - 1) * device_total
+    last_holders = min(TRUNC + 1 - last_order, device_total)
+
+    def holds_last(lat, tm):
+        return last_order + rank_of(lat, tm, lat_devices, tm_devices) <= TRUNC
+
+    def splits(phase):
+        return phases[phase][1] == slots and last_holders < device_total
+
+    if last_holders < device_total:
+
+        @pl.when(jnp.logical_not(holds_last(lat_me, tm_me)))
+        def _():
+            inbox[:, (slots - 1) * bands :] = jnp.zeros(
+                (device_total, bands, band_rows, LANES), jnp.bfloat16
+            )
+
+    def pieces_of(phase, counts, held):
         low, top = phases[phase]
+        if not held:
+            top = min(top, slots - 1)
         found = []
         shared = min(min(counts), top)
         if shared > low:
@@ -201,21 +216,27 @@
                 found.append((slot * bands + band, 1))
         return found
 
-    def blocks_of(phase, counts):
-        return sum(length for first, length in pieces_of(phase, counts))
-
-    def arriving(phase):
-        return sum(
-            (last - first) * tm_devices * blocks_of(phase, counts) for first, last, counts in runs
-        )
-
-    def holds(phase, lat, tm):
-        low, top = phases[phase]
-        rank = rank_of(lat, tm, lat_devices, tm_devices)
-        return low * device_total + rank <= TRUNC
-
-    def holders(phase):
-        return min(TRUNC + 1 - phases[phase][0] * device_total, device_total)
+    def blocks_of(phase, counts, held):
+        return sum(length for first, length in pieces_of(phase, counts, held))
+
+    def leaving(phase, counts, held):
+        kept = blocks_of(phase, counts, True) * last_holders
+        rest = blocks_of(phase, counts, False) * (device_total - last_holders)
+        return kept + rest - blocks_of(phase, counts, held)
+
+    def arriving(phase, counts, held):
+        total = sum(
+            (last - first) * tm_devices * blocks_of(phase, counts, held)
+            for first, last, counts in runs
+        )
+        return total - blocks_of(phase, counts, held)
+
+    def each_case(phase, held, act):
+        if splits(phase):
+            pl.when(held)(lambda: act(True))
+            pl.when(jnp.logical_not(held))(lambda: act(False))
+        else:
+            act(True)
 
     def wait_blocks(semaphore, count):
         if count:
@@ -263,45 +284,28 @@
             device_id_type=MESH,
         )
 
-    all_hold = [holders(phase) == device_total for phase in range(len(phases))]
-
     def send(phase):
         def send_class(counts):
             def send_to(lat, tm):
-                def go():
-                    for piece in pieces_of(phase, counts):
+                def go(held):
+                    for piece in pieces_of(phase, counts, held):
                         exchange(phase, piece, lat, tm).start()
 
-                if all_hold[phase]:
-                    go()
-                else:
-                    pl.when(holds(phase, lat, tm))(go)
-
-            if blocks_of(phase, counts):
+                each_case(phase, holds_last(lat, tm), go)
+
+            if pieces_of(phase, counts, True):
                 each_peer(send_to)
 
         each_class(send_class)
 
-    def wait_sent(phase):
-        def wait_class(counts):
-            length = blocks_of(phase, counts)
-            if all_hold[phase]:
-                wait_blocks(send_sem.at[phase], (device_total - 1) * length)
-            elif length:
-                held = holds(phase, lat_me, tm_me)
-                pl.when(held)(
-                    lambda: wait_blocks(send_sem.at[phase], (holders(phase) - 1) * length)
-                )
-                pl.when(jnp.logical_not(held))(
-                    lambda: wait_blocks(send_sem.at[phase], holders(phase) * length)
-                )
-
-        each_class(wait_class)
-
-    def wait_arrived(phase):
+    held_here = holds_last(lat_me, tm_me)
+
+    def wait_moved(phase, semaphore, amount):
         each_class(
-            lambda counts: wait_blocks(
-                recv_sem.at[phase], arriving(phase) - blocks_of(phase, counts)
+            lambda counts: each_case(
+                phase,
+                held_here,
+                lambda held: wait_blocks(semaphore.at[phase], amount(phase, counts, held)),
             )
         )
 
@@ -380,15 +384,13 @@
 
     per_share = lat_groups // share
     width = tm_devices * LANES
-    share_of = lax.broadcasted_iota(jnp.int32, (depth, width), 1) % HALF // months
-    gram_ref[...] = jnp.zeros_like(gram_ref)
-
-    def add_slot(slot):
+
+    def coefficients(slot, height):
         received = jnp.concatenate(
             [
                 jnp.concatenate(
                     [
-                        inbox[lat_device * tm_devices + tm, pl.ds(slot * bands, bands)].reshape(
+                        inbox[lat_device * tm_devices + tm, slot * bands : (slot + 1) * bands].reshape(
                             high, LANES
                         )
                         for lat_device in range(lat_devices)
@@ -399,12 +401,13 @@
             ],
             axis=1,
         )
-        first = pl.multiple_of(slot * depth, 8)
+        share_of = lax.broadcasted_iota(jnp.int32, (height, width), 1) % HALF // months
+        first = slot * depth
         merged = None
         for part in range(share):
             basis = jnp.concatenate(
                 [
-                    legendre[part * per_share + g, pl.ds(first, depth), :].astype(jnp.bfloat16)
+                    legendre[part * per_share + g, first : first + height, :].astype(jnp.bfloat16)
                     for g in range(per_share)
                 ],
                 axis=1,
@@ -414,26 +417,24 @@
         total = merged
         for part in range(1, share):
             total = total + pltpu.roll(merged, width - part * months, 1)
-        coefficients = jnp.where(share_of == 0, total, 0.0).astype(jnp.bfloat16)
-        gram_ref[...] += lax.dot_general(
-            coefficients,
-            coefficients,
-            (((0,), (0,)), ((), ())),
-            preferred_element_type=jnp.float32,
-        )
-
-    def finish(phase):
-        low, top = phases[phase]
+        return jnp.where(share_of == 0, total, 0.0).astype(jnp.bfloat16)
+
+    for phase, (low, top) in enumerate(phases):
         with jax.named_scope(f"recv{phase}"):
-            wait_arrived(phase)
+            wait_moved(phase, recv_sem, arriving)
         with jax.named_scope(f"slots{phase}"):
-            pl.loop(low, top)(add_slot)
-
-    for phase in range(len(phases)):
-        if all_hold[phase]:
-            finish(phase)
-        else:
-            pl.when(holds(phase, lat_me, tm_me))(functools.partial(finish, phase))
+            heights = [
+                min(-(-(TRUNC + 1 - slot * device_total) // 16) * 16, depth)
+                for slot in range(low, top)
+            ]
+            values = jnp.concatenate(
+                [coefficients(low + index, height) for index, height in enumerate(heights)],
+                axis=0,
+            )
+            product = lax.dot_general(
+                values, values, (((0,), (0,)), ((), ())), preferred_element_type=jnp.float32
+            )
+            gram_ref[...] = product if phase == 0 else gram_ref[...] + product
 
     gram = None
     for part in range(2):
@@ -509,7 +510,7 @@
 
     with jax.named_scope("waitsend"):
         for phase in range(len(phases)):
-            wait_sent(phase)
+            wait_moved(phase, send_sem, leaving)
 
     with jax.named_scope("owner"):
 
@@ -575,7 +576,7 @@
         dma = pltpu.SemaphoreType.DMA
         return pl.pallas_call(
             functools.partial(kernel, dims, runs),
-            out_shape=jax.ShapeDtypeStruct((months, month_total), jnp.float32),
+            out_shape=pltpu.VMEM((months, month_total), jnp.float32),
             in_specs=[hbm, hbm, hbm, hbm],
             out_specs=vmem,
             scratch_shapes=[

time: 41.3 us -> 39.2 us (0.949)
  Pallas kernels: 39.7 us -> 38.4 us
  local copies, waits for them, and re-layouts: 1.32 us -> 0.61 us
    pallas_call x1, Pallas kernels: 39.7 us -> 38.4 us  [local(): pl.pallas_call(functools.partial(kernel, dims, runs), out_shape=pltpu.VME...]
    unnamed x1, local copies, waits for them, and re-layouts: 1.32 us -> 0.61 us
where the time goes in v2:
time: 39.2 us; the launch traced here: 39 us
  Pallas kernels  38.4 us (98%)
  local copies, waits for them, and re-layouts  0.61 us (2%)
    pallas_call x1, Pallas kernels, local(): pl.pallas_call(functools.partial(kernel, dims, runs), out_shape=pltpu.VME...  38.4 us

profile of v2, /device:TPU:0, one launch (start us, length us, event | category | flops | bytes accessed | tf_op | source)
XLA Modules:
  0.0 39.0 jit_solution(8094043895799040424)
XLA Ops:
  0.0 38.4 %shard_map.46 = f32[32,64]{1,0:T(8,128)S(1)} custom-call(bf16[1024,1024]{1,0:T(8,128)(2,1)} %bitcast.1, bf16[704,1024]{1,0:T(8,128)(2,1)} %constant.6.clone.table_hbm, f32[32,16,128]{2,1,0:T(8,128)} %constant.7.clone.start_hbm, f32[3,4,128]{2,1,0:T(4,128)} %constant.8.clone.lat_hbm), custom_call_target="tpu_custom_call" | custom-call | tf_op jit(solution)/shard_map/pallas_call | solution.py:577
  38.4 0.6 %copy.6 = f32[32,64]{1,0:T(8,128)} copy(f32[32,64]{1,0:T(8,128)S(1)} %shard_map.46) | data formatting | bytes 16384

commit v3 on v2

--- a/solution.py
+++ b/solution.py
@@ -129,7 +129,8 @@
     lat_total = lat_devices * rows
     lat_groups = lat_total // LANES
     month_total = months * tm_devices
-    pieces = month_total // PIECE
+    group = months // PIECE
+    pieces = group * tm_devices
     lat_me = lax.axis_index("lat")
     tm_me = lax.axis_index("tm")
     me = lat_me * tm_devices + tm_me
@@ -453,97 +454,78 @@
             axis=1,
         )
         gram = block if gram is None else gram + block
-    local_gram[...] = gram.reshape(pieces, PIECE, month_total)
-
-    owner_lats = -(-pieces // tm_devices)
-    lat_step = max(lat_devices // 2 // owner_lats, 1)
-    first_lat = lat_devices // 4 + lat_step - 1
-
-    def owner(piece):
-        return (first_lat + (piece // tm_devices) * lat_step, piece % tm_devices)
-
-    def mine(piece):
-        lat, tm = owner(piece)
-        return (lat == lat_me) & (tm == tm_me)
-
-    def send_part(piece, source):
+    on_diagonal = lax.broadcasted_iota(jnp.int32, gram.shape, 0) == lax.broadcasted_iota(
+        jnp.int32, gram.shape, 1
+    )
+    diagonal = jnp.sum(jnp.where(on_diagonal, gram, 0.0), axis=0, keepdims=True)
+    local_gram[:, :PIECE] = gram.reshape(pieces, PIECE, month_total)
+    local_gram[:, PIECE:] = jnp.broadcast_to(diagonal[None], (pieces, 1, month_total))
+
+    first_lat = lat_me // group * group
+    place = lat_me % group
+    local_me = place * tm_devices + tm_me
+
+    def send_part(other, tm):
         return pltpu.make_async_remote_copy(
-            src_ref=local_gram.at[piece],
-            dst_ref=parts.at[source],
+            src_ref=local_gram.at[tm * group + other],
+            dst_ref=parts.at[local_me],
             send_sem=tail_sem.at[0],
             recv_sem=tail_sem.at[1],
-            device_id=owner(piece),
+            device_id=(first_lat + other, tm),
             device_id_type=MESH,
         )
 
-    def send_sum(piece, lat, tm):
+    def send_sum(lat):
         return pltpu.make_async_remote_copy(
             src_ref=own_sum,
-            dst_ref=full.at[piece],
+            dst_ref=full.at[lat_me],
             send_sem=tail_sem.at[2],
             recv_sem=tail_sem.at[3],
-            device_id=(lat, tm),
+            device_id=(lat, tm_me),
             device_id_type=MESH,
         )
 
-    def not_mine(piece):
-        return jnp.logical_not(mine(piece))
-
-    owns_any = (
-        (lat_me >= first_lat)
-        & ((lat_me - first_lat) % lat_step == 0)
-        & ((lat_me - first_lat) // lat_step * tm_devices + tm_me < pieces)
-    )
-
-    def wait_refs(index, ref):
-        pltpu.make_async_copy(ref, ref, tail_sem.at[index]).wait()
-
-    def wait_pieces(index, ref):
-        pl.when(owns_any)(lambda: wait_refs(index, ref.at[pl.ds(0, pieces - 1)]))
-        pl.when(jnp.logical_not(owns_any))(lambda: wait_refs(index, ref))
-
-    @pl.loop(0, pieces)
-    def _(piece):
-        @pl.when(not_mine(piece))
-        def _():
-            send_part(piece, me).start()
+    def wait_tail(index, ref, count):
+        if count:
+            span = ref.at[pl.ds(0, count)]
+            pltpu.make_async_copy(span, span, tail_sem.at[index]).wait()
+
+    for other in range(group):
+        for tm in range(tm_devices):
+
+            @pl.when((other != place) | (tm != tm_me))
+            def _():
+                send_part(other, tm).start()
 
     with jax.named_scope("waitsend"):
         for phase in range(len(phases)):
             wait_moved(phase, send_sem, leaving)
 
+    parts[local_me] = local_gram[tm_me * group + place]
     with jax.named_scope("owner"):
-
-        @pl.loop(0, pieces)
-        def _(piece):
-            @pl.when(mine(piece))
-            def _():
-                parts[me] = local_gram[piece]
-                wait_refs(1, parts.at[pl.ds(0, device_total - 1)])
-                total = jnp.sum(parts[...], axis=0)
-                own_sum[...] = total
-                full[piece] = total
-                each_peer(lambda lat, tm: send_sum(piece, lat, tm).start())
+        wait_tail(1, parts, pieces - 1)
+    total = jnp.sum(parts[...], axis=0)
+    own_sum[...] = total
+    full[lat_me] = total
+
+    @pl.loop(1, lat_devices)
+    def _(step):
+        send_sum(lax.rem(lat_me + step, lat_devices)).start()
 
     with jax.named_scope("waitsum"):
-
-        wait_pieces(3, full)
+        wait_tail(3, full, lat_devices - 1)
 
     with jax.named_scope("norm"):
-        gram = full[...].reshape(month_total, month_total)
-        on_diagonal = lax.broadcasted_iota(jnp.int32, gram.shape, 0) == lax.broadcasted_iota(
-            jnp.int32, gram.shape, 1
-        )
-        trace = jnp.sum(jnp.where(on_diagonal, gram, 0.0))
-        here = full[pl.ds(tm_me * (months // PIECE), months // PIECE)].reshape(months, month_total)
+        sums = full[:group]
+        for block in range(group, lat_devices, group):
+            sums = sums + full[block : block + group]
+        trace = jnp.sum(sums[0, PIECE:])
+        here = sums[:, :PIECE].reshape(months, month_total)
         out_ref[...] = month_total * here / (trace + 1e-06)
 
     with jax.named_scope("drain"):
-        wait_pieces(0, local_gram)
-
-        @pl.when(owns_any)
-        def _():
-            wait_refs(2, parts.at[pl.ds(0, device_total - 1)])
+        wait_tail(0, local_gram, pieces - 1)
+        wait_tail(2, full, lat_devices - 1)
 
 
 def solution(mesh):
@@ -589,10 +571,10 @@
                 pltpu.VMEM((device_total, slots * bands, high // bands, LANES), jnp.bfloat16),
                 pltpu.VMEM((lat_total // LANES, slot_rows * depth, LANES), jnp.float32),
                 pltpu.VMEM((width, width), jnp.float32),
-                pltpu.VMEM((pieces, PIECE, month_total), jnp.float32),
-                pltpu.VMEM((device_total, PIECE, month_total), jnp.float32),
-                pltpu.VMEM((PIECE, month_total), jnp.float32),
-                pltpu.VMEM((pieces, PIECE, month_total), jnp.float32),
+                pltpu.VMEM((pieces, PIECE + 1, month_total), jnp.float32),
+                pltpu.VMEM((pieces, PIECE + 1, month_total), jnp.float32),
+                pltpu.VMEM((PIECE + 1, month_total), jnp.float32),
+                pltpu.VMEM((lat_devices, PIECE + 1, month_total), jnp.float32),
                 dma,
                 dma((len(phases),)),
                 dma((2,)),

time: 39.2 us -> 39.4 us (level)
  no operation moved by 1% of the time
where the time goes in v3:
time: 39.4 us; the launch traced here: 39.3 us
  Pallas kernels  38.7 us (98%)
  local copies, waits for them, and re-layouts  0.61 us (2%)
    pallas_call x1, Pallas kernels, local(): pl.pallas_call(functools.partial(kernel, dims, runs), out_shape=pltpu.VME...  38.7 us

profile of v3, /device:TPU:0, one launch (start us, length us, event | category | flops | bytes accessed | tf_op | source)
XLA Modules:
  0.0 39.3 jit_solution(10919847026790833862)
XLA Ops:
  0.0 38.7 %shard_map.46 = f32[32,64]{1,0:T(8,128)S(1)} custom-call(bf16[1024,1024]{1,0:T(8,128)(2,1)} %bitcast.1, bf16[704,1024]{1,0:T(8,128)(2,1)} %constant.6.clone.table_hbm, f32[32,16,128]{2,1,0:T(8,128)} %constant.7.clone.start_hbm, f32[3,4,128]{2,1,0:T(4,128)} %constant.8.clone.lat_hbm), custom_call_target="tpu_custom_call" | custom-call | tf_op jit(solution)/shard_map/pallas_call | solution.py:559
  38.7 0.6 %copy.6 = f32[32,64]{1,0:T(8,128)} copy(f32[32,64]{1,0:T(8,128)S(1)} %shard_map.46) | data formatting | bytes 16384

commit v4 on v3

--- a/solution.py
+++ b/solution.py
@@ -87,6 +87,17 @@
     return tuple(tuple(run) for run in runs)
 
 
+def relay_routes(lat_devices, group, runs, first_top):
+    if lat_devices != 4 * group or group % 2:
+        return ()
+    routes = []
+    for source, via in ((group // 2, 0), (lat_devices - 1 - group // 2, lat_devices - 1)):
+        for first, last, counts in runs:
+            if (first, last) == (source, source + 1) and 0 < max(counts) <= first_top:
+                routes.append((source, via, counts))
+    return tuple(routes)
+
+
 def lat_table(lat_total, share):
     lat = np.arange(lat_total).reshape(lat_total // share, share).T.reshape(-1)
     theta = math.pi * (lat + 0.5) / lat_total
@@ -97,6 +108,7 @@
 def kernel(
     dims,
     runs,
+    routes,
     x_hbm,
     table_hbm,
     start_hbm,
@@ -109,6 +121,7 @@
     spread,
     outbox,
     inbox,
+    relay,
     legendre,
     gram_ref,
     local_gram,
@@ -120,6 +133,7 @@
     small_sem,
     send_sem,
     recv_sem,
+    relay_sem,
     tail_sem,
 ):
     lat_devices, tm_devices, rows, months, lon_count, slots, slot_rows, depth = dims
@@ -158,6 +172,21 @@
         )
     )
 
+    hemisphere = lat_devices // 2
+
+    def each_target(act):
+        @pl.loop(0, lat_devices)
+        def _(step):
+            if lat_devices & (lat_devices - 1):
+                lat = lax.rem(lat_me + step, lat_devices)
+            else:
+                lat = lat_me ^ ((step // 2) ^ ((step + 1) % 2 * hemisphere))
+            for tm in range(tm_devices):
+
+                @pl.when((lat != lat_me) | (tm != tm_me))
+                def _():
+                    act(lat, tm)
+
     x_copy = pltpu.make_async_copy(x_hbm, x_ref, x_sem)
     x_copy.start()
 
@@ -220,12 +249,19 @@
     def blocks_of(phase, counts, held):
         return sum(length for first, length in pieces_of(phase, counts, held))
 
-    def leaving(phase, counts, held):
+    sources = [source for source, via, counts in routes]
+
+    def relays(phase, first):
+        return phase == 0 and first in sources
+
+    def leaving(phase, first, counts, held):
+        if relays(phase, first):
+            return blocks_of(phase, counts, held) * (device_total // 2 - 1)
         kept = blocks_of(phase, counts, True) * last_holders
         rest = blocks_of(phase, counts, False) * (device_total - last_holders)
         return kept + rest - blocks_of(phase, counts, held)
 
-    def arriving(phase, counts, held):
+    def arriving(phase, first, counts, held):
         total = sum(
             (last - first) * tm_devices * blocks_of(phase, counts, held)
             for first, last, counts in runs
@@ -249,7 +285,7 @@
 
             @pl.when((lat_me >= first) & (lat_me < last))
             def _():
-                act(counts)
+                act(first, counts)
 
     def transform(phase):
         low, top = phases[phase]
@@ -285,8 +321,36 @@
             device_id_type=MESH,
         )
 
+    def across(source):
+        return hemisphere - source // hemisphere * hemisphere
+
+    def to_relay(source, via):
+        span = pl.ds(across(source) * tm_devices, hemisphere * tm_devices)
+        return pltpu.make_async_remote_copy(
+            src_ref=outbox.at[span, pl.ds(0, relay.shape[1])],
+            dst_ref=relay,
+            send_sem=relay_sem.at[0],
+            recv_sem=relay_sem.at[1],
+            device_id=(via, tm_me),
+            device_id_type=MESH,
+        )
+
+    def from_relay(source, counts):
+        @pl.loop(0, hemisphere * tm_devices)
+        def _(index):
+            for piece in pieces_of(0, counts, True):
+                span = pl.ds(*piece)
+                pltpu.make_async_remote_copy(
+                    src_ref=relay.at[index, span],
+                    dst_ref=inbox.at[source * tm_devices + tm_me, span],
+                    send_sem=relay_sem.at[2],
+                    recv_sem=recv_sem.at[0],
+                    device_id=(across(source) + index // tm_devices, index % tm_devices),
+                    device_id_type=MESH,
+                ).start()
+
     def send(phase):
-        def send_class(counts):
+        def send_class(start, counts):
             def send_to(lat, tm):
                 def go(held):
                     for piece in pieces_of(phase, counts, held):
@@ -294,8 +358,16 @@
 
                 each_case(phase, holds_last(lat, tm), go)
 
-            if pieces_of(phase, counts, True):
-                each_peer(send_to)
+            def send_near(lat, tm):
+                pl.when(lat // hemisphere == start // hemisphere)(lambda: send_to(lat, tm))
+
+            if relays(phase, start):
+                for source, via, _ in routes:
+                    if source == start:
+                        to_relay(source, via).start()
+                each_target(send_near)
+            elif pieces_of(phase, counts, True):
+                each_target(send_to)
 
         each_class(send_class)
 
@@ -303,10 +375,10 @@
 
     def wait_moved(phase, semaphore, amount):
         each_class(
-            lambda counts: each_case(
+            lambda first, counts: each_case(
                 phase,
                 held_here,
-                lambda held: wait_blocks(semaphore.at[phase], amount(phase, counts, held)),
+                lambda held: wait_blocks(semaphore.at[phase], amount(phase, first, counts, held)),
             )
         )
 
@@ -383,6 +455,17 @@
             unroll=7,
         )
 
+    def wait_relay(index, ref):
+        pltpu.make_async_copy(ref, ref, relay_sem.at[index]).wait()
+
+    with jax.named_scope("relay"):
+        for source, via, counts in routes:
+
+            @pl.when(lat_me == via)
+            def _():
+                wait_relay(1, relay)
+                from_relay(source, counts)
+
     per_share = lat_groups // share
     width = tm_devices * LANES
 
@@ -500,6 +583,17 @@
     with jax.named_scope("waitsend"):
         for phase in range(len(phases)):
             wait_moved(phase, send_sem, leaving)
+        for source, via, counts in routes:
+
+            @pl.when(lat_me == source)
+            def _():
+                wait_relay(0, relay)
+
+            @pl.when(lat_me == via)
+            def _():
+                wait_blocks(
+                    relay_sem.at[2], hemisphere * tm_devices * blocks_of(0, counts, True)
+                )
 
     parts[local_me] = local_gram[tm_me * group + place]
     with jax.named_scope("owner"):
@@ -553,11 +647,13 @@
         runs = needed_slots(lat_devices, device_total, slots, rows, bands)
         phases = phase_bounds(slots)
         longest = max(top - low for low, top in phases)
+        routes = relay_routes(lat_devices, months // PIECE, runs, phases[0][1])
+        carried = max([max(counts) * bands for source, via, counts in routes] + [1])
         hbm = pl.BlockSpec(memory_space=pl.ANY)
         vmem = pl.BlockSpec(memory_space=pltpu.VMEM)
         dma = pltpu.SemaphoreType.DMA
         return pl.pallas_call(
-            functools.partial(kernel, dims, runs),
+            functools.partial(kernel, dims, runs, routes),
             out_shape=pltpu.VMEM((months, month_total), jnp.float32),
             in_specs=[hbm, hbm, hbm, hbm],
             out_specs=vmem,
@@ -569,6 +665,7 @@
                 pltpu.VMEM((device_total * longest * high, LANES), jnp.float32),
                 pltpu.VMEM((device_total, slots * bands, high // bands, LANES), jnp.bfloat16),
                 pltpu.VMEM((device_total, slots * bands, high // bands, LANES), jnp.bfloat16),
+                pltpu.VMEM((device_total // 2, carried, high // bands, LANES), jnp.bfloat16),
                 pltpu.VMEM((lat_total // LANES, slot_rows * depth, LANES), jnp.float32),
                 pltpu.VMEM((width, width), jnp.float32),
                 pltpu.VMEM((pieces, PIECE + 1, month_total), jnp.float32),
@@ -580,6 +677,7 @@
                 dma((2,)),
                 dma((len(phases),)),
                 dma((len(phases),)),
+                dma((3,)),
                 dma((4,)),
             ],
             compiler_params=pltpu.CompilerParams(

time: 39.4 us -> 37.2 us (0.944)
  Pallas kernels: 38.7 us -> 36.4 us
    pallas_call x1, Pallas kernels: 38.7 us -> 36.4 us  [local(): pl.pallas_call(functools.partial(kernel, dims, runs, routes), out_shape=p...]
where the time goes in v4:
time: 37.2 us; the launch traced here: 37 us
  Pallas kernels  36.4 us (98%)
  local copies, waits for them, and re-layouts  0.61 us (2%)
    pallas_call x1, Pallas kernels, local(): pl.pallas_call(functools.partial(kernel, dims, runs, routes), out_shape=p...  36.4 us

profile of v4, /device:TPU:0, one launch (start us, length us, event | category | flops | bytes accessed | tf_op | source)
XLA Modules:
  0.0 37.0 jit_solution(14002288778523468540)
XLA Ops:
  0.0 36.4 %shard_map.46 = f32[32,64]{1,0:T(8,128)S(1)} custom-call(bf16[1024,1024]{1,0:T(8,128)(2,1)} %bitcast.1, bf16[704,1024]{1,0:T(8,128)(2,1)} %constant.6.clone.table_hbm, f32[32,16,128]{2,1,0:T(8,128)} %constant.7.clone.start_hbm, f32[3,4,128]{2,1,0:T(4,128)} %constant.8.clone.lat_hbm), custom_call_target="tpu_custom_call" | custom-call | tf_op jit(solution)/shard_map/pallas_call | solution.py:655
  36.4 0.6 %copy.6 = f32[32,64]{1,0:T(8,128)} copy(f32[32,64]{1,0:T(8,128)S(1)} %shard_map.46) | data formatting | bytes 16384

commit v5 on v4

--- a/solution.py
+++ b/solution.py
@@ -14,6 +14,7 @@
 HALF = 64
 PIECE = 8
 PHASES = 3
+CHUNKS = 2
 MESH = pl.DeviceIdType.MESH
 
 
@@ -133,6 +134,7 @@
     small_sem,
     send_sem,
     recv_sem,
+    far_sem,
     relay_sem,
     tail_sem,
 ):
@@ -166,11 +168,52 @@
                 act(lat_me, tm)
 
     barrier = pltpu.get_barrier_semaphore()
-    each_peer(
-        lambda lat, tm: pl.semaphore_signal(
-            barrier, inc=1, device_id=(lat, tm), device_id_type=MESH
-        )
-    )
+    staged = lat_devices == 4 * group and len(phase_bounds(slots)) > 1
+    block_me = lat_me // group
+
+    def near(lat):
+        return jnp.abs(lat // group - block_me) <= 1
+
+    def greet(lat, tm):
+        def signal():
+            pl.semaphore_signal(barrier, inc=1, device_id=(lat, tm), device_id_type=MESH)
+
+        if staged:
+            pl.when(near(lat))(signal)
+        else:
+            signal()
+
+    each_peer(greet)
+
+    def pass_on(index, block, other):
+        @pl.when(block_me == block)
+        def _():
+            pl.semaphore_signal(
+                far_sem.at[index],
+                inc=1,
+                device_id=(lat_me + (other - block) * group, tm_me),
+                device_id_type=MESH,
+            )
+
+    def wait_near():
+        if not staged:
+            pl.semaphore_wait(barrier, device_total - 1)
+            return
+        inner = (block_me == 1) | (block_me == 2)
+        size = group * tm_devices
+        pl.when(inner)(lambda: pl.semaphore_wait(barrier, 3 * size - 1))
+        pl.when(jnp.logical_not(inner))(lambda: pl.semaphore_wait(barrier, 2 * size - 1))
+        for block, other in ((1, 0), (1, 2), (2, 1), (2, 3)):
+            pass_on(0, block, other)
+
+    def wait_far():
+        pl.semaphore_wait(far_sem.at[0], 1)
+        pass_on(1, 1, 0)
+        pass_on(1, 2, 3)
+
+        @pl.when((block_me == 0) | (block_me == 3))
+        def _():
+            pl.semaphore_wait(far_sem.at[1], 1)
 
     hemisphere = lat_devices // 2
 
@@ -187,16 +230,20 @@
                 def _():
                     act(lat, tm)
 
-    x_copy = pltpu.make_async_copy(x_hbm, x_ref, x_sem)
-    x_copy.start()
+    chunk = rows * months // CHUNKS
+
+    def x_copy(index):
+        span = pl.ds(index * chunk, chunk)
+        return pltpu.make_async_copy(x_hbm.at[span], x_ref.at[span], x_sem.at[index])
 
     def table_copy(phase):
         low, top = phases[phase]
         span = pl.ds(2 * device_total * low, 2 * device_total * (top - low))
         return pltpu.make_async_copy(table_hbm.at[span], table_ref.at[span], table_sem.at[phase])
 
-    for phase in range(len(phases)):
-        table_copy(phase).start()
+    table_copy(0).start()
+    for index in range(CHUNKS):
+        x_copy(index).start()
 
     start_copy = pltpu.make_async_copy(start_hbm.at[me], start_ref, small_sem.at[0])
     start_copy.start()
@@ -292,19 +339,26 @@
         group_rows = device_total * (top - low)
         lower = lax.broadcasted_iota(jnp.int32, (group_rows, LANES), 1) < HALF
         table_copy(phase).wait()
-        values = lax.dot_general(
-            table_ref[2 * device_total * low : 2 * device_total * top],
-            x_ref[...],
-            (((1,), (1,)), ((), ())),
-            preferred_element_type=jnp.float32,
-        )
-        for block in range(rows * months // LANES):
-            cosine = values[:group_rows, block * LANES : (block + 1) * LANES]
-            sine = values[group_rows:, block * LANES : (block + 1) * LANES]
-            even = jnp.where(lower, cosine, pltpu.roll(sine, HALF, 1))
-            odd = jnp.where(lower, pltpu.roll(cosine, HALF, 1), sine)
-            spread[pl.ds(2 * block, group_rows, stride=high), :] = even
-            spread[pl.ds(2 * block + 1, group_rows, stride=high), :] = odd
+        for index in range(CHUNKS):
+            if phase == 0:
+                x_copy(index).wait()
+                if index == 0:
+                    for later in range(1, len(phases)):
+                        table_copy(later).start()
+            values = lax.dot_general(
+                table_ref[2 * device_total * low : 2 * device_total * top],
+                x_ref[index * chunk : (index + 1) * chunk],
+                (((1,), (1,)), ((), ())),
+                preferred_element_type=jnp.float32,
+            )
+            for block in range(chunk // LANES):
+                cosine = values[:group_rows, block * LANES : (block + 1) * LANES]
+                sine = values[group_rows:, block * LANES : (block + 1) * LANES]
+                even = jnp.where(lower, cosine, pltpu.roll(sine, HALF, 1))
+                odd = jnp.where(lower, pltpu.roll(cosine, HALF, 1), sine)
+                row = 2 * (index * chunk // LANES + block)
+                spread[pl.ds(row, group_rows, stride=high), :] = even
+                spread[pl.ds(row + 1, group_rows, stride=high), :] = odd
         packed = spread[: group_rows * high].astype(jnp.bfloat16)
         outbox[:, low * bands : top * bands] = packed.reshape(
             device_total, (top - low) * bands, band_rows, LANES
@@ -349,9 +403,15 @@
                     device_id_type=MESH,
                 ).start()
 
-    def send(phase):
+    def send(phase, reach=None):
         def send_class(start, counts):
             def send_to(lat, tm):
+                if reach is None:
+                    send_one(lat, tm)
+                else:
+                    pl.when(near(lat) == reach)(lambda: send_one(lat, tm))
+
+            def send_one(lat, tm):
                 def go(held):
                     for piece in pieces_of(phase, counts, held):
                         exchange(phase, piece, lat, tm).start()
@@ -361,6 +421,8 @@
             def send_near(lat, tm):
                 pl.when(lat // hemisphere == start // hemisphere)(lambda: send_to(lat, tm))
 
+            if relays(phase, start) and reach is False:
+                return
             if relays(phase, start):
                 for source, via, _ in routes:
                     if source == start:
@@ -382,16 +444,32 @@
             )
         )
 
-    with jax.named_scope("xwait"):
-        x_copy.wait()
     for phase in range(len(phases)):
         with jax.named_scope(f"transform{phase}"):
             transform(phase)
         if phase == 0:
             with jax.named_scope("barrier"):
-                pl.semaphore_wait(barrier, device_total - 1)
+                wait_near()
+        if phase == 1 and staged:
+            with jax.named_scope("far"):
+                wait_far()
+            send(0, False)
         with jax.named_scope(f"send{phase}"):
-            send(phase)
+            if phase == 0 and staged:
+                send(0, True)
+            else:
+                send(phase)
+
+    def wait_relay(index, ref):
+        pltpu.make_async_copy(ref, ref, relay_sem.at[index]).wait()
+
+    with jax.named_scope("relay"):
+        for source, via, counts in routes:
+
+            @pl.when(lat_me == via)
+            def _():
+                wait_relay(1, relay)
+                from_relay(source, counts)
 
     inbox[me] = outbox[me]
 
@@ -454,17 +532,6 @@
             (current, [zero] * len(current), [zero] * halves),
             unroll=7,
         )
-
-    def wait_relay(index, ref):
-        pltpu.make_async_copy(ref, ref, relay_sem.at[index]).wait()
-
-    with jax.named_scope("relay"):
-        for source, via, counts in routes:
-
-            @pl.when(lat_me == via)
-            def _():
-                wait_relay(1, relay)
-                from_relay(source, counts)
 
     per_share = lat_groups // share
     width = tm_devices * LANES
@@ -672,11 +739,12 @@
                 pltpu.VMEM((pieces, PIECE + 1, month_total), jnp.float32),
                 pltpu.VMEM((PIECE + 1, month_total), jnp.float32),
                 pltpu.VMEM((lat_devices, PIECE + 1, month_total), jnp.float32),
-                dma,
+                dma((CHUNKS,)),
                 dma((len(phases),)),
                 dma((2,)),
                 dma((len(phases),)),
                 dma((len(phases),)),
+                pltpu.SemaphoreType.REGULAR((2,)),
                 dma((3,)),
                 dma((4,)),
             ],

time: 37.2 us -> 36.5 us (0.981)
  Pallas kernels: 36.4 us -> 35.8 us
    pallas_call x1, Pallas kernels: 36.4 us -> 35.8 us  [local(): pl.pallas_call(functools.partial(kernel, dims, runs, routes), out_shape=p...]
where the time goes in v5:
time: 36.5 us; the launch traced here: 36.4 us
  Pallas kernels  35.8 us (98%)
  local copies, waits for them, and re-layouts  0.61 us (2%)
    pallas_call x1, Pallas kernels, local(): pl.pallas_call(functools.partial(kernel, dims, runs, routes), out_shape=p...  35.8 us

profile of v5, /device:TPU:0, one launch (start us, length us, event | category | flops | bytes accessed | tf_op | source)
XLA Modules:
  0.0 36.4 jit_solution(13988640814755545712)
XLA Ops:
  0.0 35.8 %shard_map.46 = f32[32,64]{1,0:T(8,128)S(1)} custom-call(bf16[1024,1024]{1,0:T(8,128)(2,1)} %bitcast.1, bf16[704,1024]{1,0:T(8,128)(2,1)} %constant.6.clone.table_hbm, f32[32,16,128]{2,1,0:T(8,128)} %constant.7.clone.start_hbm, f32[3,4,128]{2,1,0:T(4,128)} %constant.8.clone.lat_hbm), custom_call_target="tpu_custom_call" | custom-call | tf_op jit(solution)/shard_map/pallas_call | solution.py:722
  35.8 0.6 %copy.6 = f32[32,64]{1,0:T(8,128)} copy(f32[32,64]{1,0:T(8,128)S(1)} %shard_map.46) | data formatting | bytes 16384

commit v6 on v5

--- a/solution.py
+++ b/solution.py
@@ -554,17 +554,24 @@
         )
         share_of = lax.broadcasted_iota(jnp.int32, (height, width), 1) % HALF // months
         first = slot * depth
-        merged = None
-        for part in range(share):
-            basis = jnp.concatenate(
-                [
-                    legendre[part * per_share + g, first : first + height, :].astype(jnp.bfloat16)
-                    for g in range(per_share)
-                ],
-                axis=1,
-            )
-            product = jnp.dot(basis, received, preferred_element_type=jnp.float32)
-            merged = product if part == 0 else jnp.where(share_of == part, product, merged)
+        basis = jnp.concatenate(
+            [
+                jnp.concatenate(
+                    [
+                        legendre[part * per_share + g, first : first + height, :]
+                        for g in range(per_share)
+                    ],
+                    axis=1,
+                )
+                for part in range(share)
+            ],
+            axis=0,
+        ).astype(jnp.bfloat16)
+        product = jnp.dot(basis, received, preferred_element_type=jnp.float32)
+        merged = product[:height]
+        for part in range(1, share):
+            part_product = product[part * height : (part + 1) * height]
+            merged = jnp.where(share_of == part, part_product, merged)
         total = merged
         for part in range(1, share):
             total = total + pltpu.roll(merged, width - part * months, 1)

time: 36.5 us -> 36.4 us (level)
  no operation moved by 1% of the time
where the time goes in v6:
time: 36.4 us; the launch traced here: 36.3 us
  Pallas kernels  35.7 us (98%)
  local copies, waits for them, and re-layouts  0.61 us (2%)
    pallas_call x1, Pallas kernels, local(): pl.pallas_call(functools.partial(kernel, dims, runs, routes), out_shape=p...  35.7 us

profile of v6, /device:TPU:0, one launch (start us, length us, event | category | flops | bytes accessed | tf_op | source)
XLA Modules:
  0.0 36.3 jit_solution(11021011387241291194)
XLA Ops:
  0.0 35.7 %shard_map.46 = f32[32,64]{1,0:T(8,128)S(1)} custom-call(bf16[1024,1024]{1,0:T(8,128)(2,1)} %bitcast.1, bf16[704,1024]{1,0:T(8,128)(2,1)} %constant.6.clone.table_hbm, f32[32,16,128]{2,1,0:T(8,128)} %constant.7.clone.start_hbm, f32[3,4,128]{2,1,0:T(4,128)} %constant.8.clone.lat_hbm), custom_call_target="tpu_custom_call" | custom-call | tf_op jit(solution)/shard_map/pallas_call | solution.py:729
  35.7 0.6 %copy.6 = f32[32,64]{1,0:T(8,128)} copy(f32[32,64]{1,0:T(8,128)S(1)} %shard_map.46) | data formatting | bytes 16384
